TPU v7x, 256 devices: a whole 4x4x8 slice. The times are simulated.
256 devices in a mesh: dp: 16 (over x_lo, z), fsdp: 16 (over y, x_hi, core).
Axes of the slice: x: 4 (x_hi: 2, x_lo: 2; x = x_hi * 2 + x_lo), y: 4, z: 8, core: 2. Of those that a mesh axis runs over, the one named last changes fastest.
Arguments:
- hidden_states: bfloat16 [32768, 8192], P(('dp', 'fsdp')), may hold values from -450 to 450
- gain: float32 [8192], replicated, may hold values from 0.1 to 1.9
- key_weight: bfloat16 [8192, 512], P('fsdp'), may hold values from -0.0625 to 0.0625
- key_cotangent: bfloat16 [32768, 512], P(('dp', 'fsdp')), may hold values from -18 to 18
- bucket: int32 [5, 32768], P(None, 'fsdp'), may hold values from 0 to 255
- sign_bits: int32 [5, 32768], P(None, 'fsdp'), may hold values from 0 to 1
- momentum: float32 [16, 5, 32768], P('fsdp', None, 'dp'), may hold values from -12 to 12
- error: float32 [16, 5, 32768], P('fsdp', None, 'dp'), may hold values from -12 to 12
Outputs:
- hidden_grad: bfloat16 [32768, 8192], P(('dp', 'fsdp'))
- momentum_new: float32 [16, 5, 32768], P('fsdp', None, 'dp')
- error_new: float32 [16, 5, 32768], P('fsdp', None, 'dp')
- update: float32 [8192, 512], P('fsdp')
All inputs are finite; a program needn't handle non-finite values.
Results may differ from a plain program's by a relative error of at most 0.0095.
Values may be sent and summed in bfloat16 or wider, within the bound.
A program may use at most 128 MiB of HBM per device.

v0:
```python
import math
import jax
import jax.numpy as jnp
from jax import lax
from jax.sharding import PartitionSpec as P

ROWS = 5
NBB = 256
BLOCK = 128
EPS = 1e-05
DECAY = 0.9
THRESHOLD = 1.0


def normalize(states, gain):
    values = states.astype(jnp.float32)
    inverse_rms = lax.rsqrt(jnp.mean(values * values, axis=1, keepdims=True) + EPS)
    normed = values * inverse_rms
    return (normed, inverse_rms, (normed * gain).astype(jnp.bfloat16))


def norm_backward(input_grad, gain, normed, inverse_rms):
    scaled = input_grad.astype(jnp.float32) * gain
    mean_term = jnp.mean(scaled * normed, axis=1, keepdims=True)
    return (inverse_rms * (scaled - normed * mean_term)).astype(jnp.bfloat16)


def split_product(selector, values, numbers):
    upper = values.astype(jnp.bfloat16)
    lower = (values - upper.astype(jnp.float32)).astype(jnp.bfloat16)
    first = lax.dot_general(selector, upper, numbers, preferred_element_type=jnp.float32)
    return first + lax.dot_general(selector, lower, numbers, preferred_element_type=jnp.float32)


def middle_three(first, second, third):
    return jnp.maximum(jnp.minimum(first, second), jnp.minimum(jnp.maximum(first, second), third))


def middle_five(items):
    upper_pair = jnp.minimum(jnp.maximum(items[0], items[1]), jnp.maximum(items[2], items[3]))
    lower_pair = jnp.maximum(jnp.minimum(items[0], items[1]), jnp.minimum(items[2], items[3]))
    return middle_three(items[4], upper_pair, lower_pair)


def on_device(hidden_states, gain, key_weight, key_cotangent, bucket, sign_bits, momentum, error):
    normed, inverse_rms, inputs = normalize(hidden_states, gain)
    fsdp_count = lax.axis_size("fsdp")
    dp_count = lax.axis_size("dp")
    local_rows = key_weight.shape[0]
    grad_scale = 1.0 / math.sqrt(inputs.shape[0] * fsdp_count)
    contract_last = (((1,), (1,)), ((), ()))
    contract_first = (((0,), (0,)), ((), ()))
    contract_plain = (((1,), (0,)), ((), ()))
    input_grad = lax.dot_general(
        key_cotangent,
        lax.all_gather(key_weight, "fsdp", axis=0, tiled=True),
        contract_last,
        preferred_element_type=jnp.float32,
    ).astype(jnp.bfloat16)
    weight_grad = lax.psum_scatter(
        lax.dot_general(inputs, key_cotangent, contract_first, preferred_element_type=jnp.float32),
        "fsdp",
        scatter_dimension=0,
        tiled=True,
    )
    hidden_grad = norm_backward(input_grad, gain, normed, inverse_rms)
    blocks = (weight_grad * grad_scale).reshape(-1, BLOCK)
    signs = (2 * sign_bits - 1).astype(jnp.bfloat16)
    sign_values = (2 * sign_bits - 1).astype(jnp.float32)
    zero_sel = jnp.zeros((), jnp.bfloat16)
    bucket_ids = lax.broadcasted_iota(jnp.int32, (NBB, 1), 0)
    local_table = jnp.stack(
        [
            split_product(
                jnp.where(
                    bucket[row_index][None, :] == bucket_ids, signs[row_index][None, :], zero_sel
                ),
                blocks,
                contract_plain,
            )
            for row_index in range(ROWS)
        ]
    ).reshape(1, ROWS, NBB * BLOCK)
    share = momentum.shape[2]
    offset = lax.axis_index("dp") * share
    total = lax.psum(local_table, "dp")
    momentum_all, error_all = (
        lax.all_gather(momentum, "dp", axis=2, tiled=True),
        lax.all_gather(error, "dp", axis=2, tiled=True),
    )
    momentum_all = DECAY * momentum_all + total / dp_count
    error_all = error_all + momentum_all
    momentum_new = lax.dynamic_slice_in_dim(momentum_all, offset, share, 2)
    error_mid = lax.dynamic_slice_in_dim(error_all, offset, share, 2)
    error_rows = error_all.reshape(ROWS, NBB, BLOCK)
    reads = [
        error_rows[row_index][bucket[row_index]] * sign_values[row_index][:, None]
        for row_index in range(ROWS)
    ]
    estimate = middle_five(reads)
    update = estimate - jnp.clip(estimate, -THRESHOLD, THRESHOLD)
    share_buckets = share // BLOCK
    share_ids = bucket_ids[:share_buckets] + lax.axis_index("dp") * share_buckets
    sketched = jnp.stack(
        [
            split_product(
                jnp.where(
                    bucket[row_index][None, :] == share_ids, signs[row_index][None, :], zero_sel
                ),
                update,
                contract_plain,
            )
            for row_index in range(ROWS)
        ]
    ).reshape(1, ROWS, share)
    error_new = error_mid - sketched
    return (hidden_grad, momentum_new, error_new, update.reshape(local_rows, -1))


def solution(mesh):
    in_specs = (
        P(("dp", "fsdp"), None),
        P(),
        P("fsdp", None),
        P(("dp", "fsdp"), None),
        P(None, "fsdp"),
        P(None, "fsdp"),
        P("fsdp", None, "dp"),
        P("fsdp", None, "dp"),
    )
    out_specs = (
        P(("dp", "fsdp"), None),
        P("fsdp", None, "dp"),
        P("fsdp", None, "dp"),
        P("fsdp", None),
    )
    return jax.shard_map(
        on_device, mesh=mesh, in_specs=in_specs, out_specs=out_specs, check_vma=False
    )
```

profile of v0, /device:TPU:8, one launch (start us, length us, event | category | flops | bytes accessed | tf_op | source)
XLA Modules:
  0.0 459.5 jit_solution(4730571802656826122)
XLA Ops:
  7.2 0.7 all-gather.2.cloned.1.call-update
  8.0 2.1 fusion.10
  10.1 8.2 %fusion.11 = f32[8192,512]{1,0:T(8,128)} fusion(bf16[128,512]{1,0:T(8,128)(2,1)S(1)} %copy-done, bf16[128,8192]{1,0:T(8,128)(2,1)S(1)} %copy-done.1, f32[8192]{0:T(1024)S(1)} %copy-done.18, f32[128]{0:T(128)S(1)} %add_rsqrt_fusion), kind=kOutput, calls=%fused_computation.19 | convolution fusion | flops 1077936128 | bytes 19038720 | tf_op jit(solution)/shard_map/dot_general | solution.py:61
  18.4 0.7 copy-done.26
  19.8 1.0 mul.191
  20.8 1.0 mul.195
  21.8 1.0 mul.199
  22.7 1.0 mul.203
  23.7 1.0 mul.207
  28.5 42.3 %all_gather.10 = f32[1,5,32768]{2,0,1:T(1,128)} all-gather(f32[1,5,2048]{2,0,1:T(1,128)S(1)} %copy-done.28), channel_id=1, replica_groups=mesh['dp'=16,'fsdp'=16] {'dp'}, dimensions={2}, use_global_device_ids=true | all-gather | bytes 696320 | tf_op jit(solution)/shard_map/all_gather | solution.py:88
  70.8 36.0 %all_gather.11 = f32[1,5,32768]{2,0,1:T(1,128)} all-gather(f32[1,5,2048]{2,0,1:T(1,128)S(1)} %copy-done.29), channel_id=1, replica_groups=mesh['dp'=16,'fsdp'=16] {'dp'}, dimensions={2}, use_global_device_ids=true | all-gather | bytes 696320 | tf_op jit(solution)/shard_map/all_gather | solution.py:89
  106.9 9.1 %fusion.5 = (f32[128]{0:T(128)S(1)}, f32[128,8192]{1,0:T(8,128)}) fusion(bf16[128,8192]{1,0:T(8,128)(2,1)S(1)} %copy-done.1, f32[128]{0:T(128)S(1)} %add_rsqrt_fusion, f32[8192]{0:T(1024)S(1)} %copy-done.18, bf16[128,512]{1,0:T(8,128)(2,1)S(1)} %copy-done, bf16[8192,512]{1,0:T(8,128)(2,1)} %all-gather.2.cloned.1.call-done), kind=kOutput, calls=%fused_computation.13 | convolution fusion | flops 1081081728 | bytes 14844928 | tf_op jit(solution)/shard_map/dot_general | solution.py:54
  116.5 133.0 %reduce-scatter.2.cloned.1.call-done = f32[512,512]{1,0:T(8,128)} async-done(((f32[8192,512]{1,0:T(8,128)}), f32[512,512]{1,0:T(8,128)}) %reduce-scatter.2.cloned.1.call-update) | async-done | bytes 1048592 | tf_op jit(solution)/shard_map/reduce_scatter | solution.py:60
  249.6 2.3 broadcast_multiply_fusion
  251.9 1.3 reshape.223
  257.8 0.8 copy-done.17
  258.7 4.5 fusion.8
  263.2 131.6 %all-reduce.2.cloned.1.call-done = f32[1,5,32768]{2,0,1:T(1,128)} async-done(((f32[1,5,32768]{2,0,1:T(1,128)}), f32[1,5,32768]{2,0,1:T(1,128)}) %all-reduce.2.cloned.1.call-update) | async-done | bytes 655376 | tf_op jit(solution)/shard_map/psum | solution.py:86
  394.7 3.5 fusion.153
  398.3 5.7 %gather_fusion = f32[2048,128]{1,0:T(8,128)S(1)} fusion(f32[256,128]{1,0:T(8,128)S(1)} %bitcast.114, s32[2048]{0:T(1024)S(1)} %copy-done.48), kind=kCustom, calls=%fused_computation | custom fusion | bytes 2105344 | tf_op jit(solution)/shard_map/gather | solution.py:97
  404.0 1.2 gather.30
  405.2 5.5 %gather_fusion.1 = f32[2048,128]{1,0:T(8,128)S(1)} fusion(f32[256,128]{1,0:T(8,128)S(1)} %bitcast.113, s32[2048]{0:T(1024)S(1)} %copy-done.47), kind=kCustom, calls=%fused_computation.1 | custom fusion | bytes 2105344 | tf_op jit(solution)/shard_map/gather | solution.py:97
  410.7 1.1 gather.31
  411.8 7.6 %gather_fusion.2 = f32[2048,128]{1,0:T(8,128)} fusion(f32[256,128]{1,0:T(8,128)S(1)} %bitcast.112, s32[2048]{0:T(1024)S(1)} %copy-done.46), kind=kCustom, calls=%fused_computation.2 | custom fusion | bytes 2105344 | tf_op jit(solution)/shard_map/gather | solution.py:97
  419.4 2.4 gather.32
  421.8 6.4 %gather_fusion.3 = f32[2048,128]{1,0:T(8,128)S(1)} fusion(f32[256,128]{1,0:T(8,128)S(1)} %bitcast.111, s32[2048]{0:T(1024)} %broadcast_clamp_fusion.1), kind=kCustom, calls=%fused_computation.3 | custom fusion | bytes 2105344 | tf_op jit(solution)/shard_map/gather | solution.py:97
  428.2 1.3 gather.33
  429.5 7.6 %gather_fusion.4 = f32[2048,128]{1,0:T(8,128)} fusion(f32[256,128]{1,0:T(8,128)S(1)} %bitcast.110, s32[2048]{0:T(1024)S(1)} %copy-done.45), kind=kCustom, calls=%fused_computation.4 | custom fusion | bytes 2105344 | tf_op jit(solution)/shard_map/gather | solution.py:97
  437.2 2.5 gather.34
  439.8 3.5 subtract_convert_fusion
  445.9 1.5 dynamic-slice_subtract_fusion
  450.7 2.3 clamp_subtract_fusion
  (154 shorter events, 15.4 us)
Async XLA Ops:
  7.2 2.9 copy-start
  7.2 99.7 %all-gather.2.cloned.1.call-start = ((), (), s32[]{:S(2)}) async-start(), calls=%async_computation.1 | async-start | bytes 8912896 | tf_op jit(solution)/shard_map/all_gather | solution.py:56
  7.9 241.6 %reduce-scatter.2.cloned.1.call-start = ((), (), s32[]{:S(2)}) async-start(), calls=%async_computation.2 | async-start | bytes 17825792 | tf_op jit(solution)/shard_map/reduce_scatter | solution.py:60
  10.1 96.8 %copy-start.49 = (f32[128]{0:T(128)}, f32[128]{0:T(128)S(1)}, u32[]{:S(2)}) copy-start(f32[128]{0:T(128)S(1)} %add_rsqrt_fusion) | copy-start | bytes 1540
  18.3 7.1 %copy-start.19 = (s32[5,2048]{1,0:T(8,128)S(1)}, s32[5,2048]{1,0:T(8,128)}, u32[]{:S(2)}) copy-start(s32[5,2048]{1,0:T(8,128)} %param.12) | copy-start | bytes 122884
  18.3 10.2 %copy-start.28 = (f32[1,5,2048]{2,0,1:T(1,128)S(1)}, f32[1,5,2048]{2,0,1:T(1,128)}, u32[]{:S(2)}) copy-start(f32[1,5,2048]{2,0,1:T(1,128)} %param.14) | copy-start | bytes 122884
  18.3 52.5 %copy-start.29 = (f32[1,5,2048]{2,0,1:T(1,128)S(1)}, f32[1,5,2048]{2,0,1:T(1,128)}, u32[]{:S(2)}) copy-start(f32[1,5,2048]{2,0,1:T(1,128)} %param.15) | copy-start | bytes 122884
  18.3 376.4 %all-reduce.2.cloned.1.call-start = ((), (), s32[]{:S(2)}) async-start(), calls=%async_computation.3 | async-start | bytes 1310720 | tf_op jit(solution)/shard_map/psum | solution.py:86
  25.4 228.4 %copy-start.32 = (bf16[2048]{0:T(1024)(128)(2,1)}, bf16[2048]{0:T(1024)(128)(2,1)S(1)}, u32[]{:S(2)}) copy-start(bf16[2048]{0:T(1024)(128)(2,1)S(1)} %get-tuple-element.12) | copy-start | bytes 12292
  25.4 229.2 %copy-start.30 = (bf16[2048]{0:T(1024)(128)(2,1)}, bf16[2048]{0:T(1024)(128)(2,1)S(1)}, u32[]{:S(2)}) copy-start(bf16[2048]{0:T(1024)(128)(2,1)S(1)} %get-tuple-element.13) | copy-start | bytes 12292
  25.4 230.1 %copy-start.34 = (bf16[2048]{0:T(1024)(128)(2,1)}, bf16[2048]{0:T(1024)(128)(2,1)S(1)}, u32[]{:S(2)}) copy-start(bf16[2048]{0:T(1024)(128)(2,1)S(1)} %get-tuple-element.11) | copy-start | bytes 12292
  25.4 231.0 %copy-start.36 = (bf16[2048]{0:T(1024)(128)(2,1)}, bf16[2048]{0:T(1024)(128)(2,1)S(1)}, u32[]{:S(2)}) copy-start(bf16[2048]{0:T(1024)(128)(2,1)S(1)} %get-tuple-element.10) | copy-start | bytes 12292
  25.4 231.8 %copy-start.38 = (bf16[2048]{0:T(1024)(128)(2,1)}, bf16[2048]{0:T(1024)(128)(2,1)S(1)}, u32[]{:S(2)}) copy-start(bf16[2048]{0:T(1024)(128)(2,1)S(1)} %get-tuple-element.9) | copy-start | bytes 12292
  106.8 148.7 %copy-start.20 = (s32[1,2048]{1,0:T(1,128)}, s32[1,2048]{1,0:T(1,128)S(1)}, u32[]{:S(2)}) copy-start(s32[1,2048]{1,0:T(1,128)S(1)} %get-tuple-element.38) | copy-start | bytes 24580
  106.8 149.6 %copy-start.22 = (s32[1,2048]{1,0:T(1,128)}, s32[1,2048]{1,0:T(1,128)S(1)}, u32[]{:S(2)}) copy-start(s32[1,2048]{1,0:T(1,128)S(1)} %get-tuple-element.41) | copy-start | bytes 24580
  106.8 150.4 %copy-start.24 = (s32[1,2048]{1,0:T(1,128)}, s32[1,2048]{1,0:T(1,128)S(1)}, u32[]{:S(2)}) copy-start(s32[1,2048]{1,0:T(1,128)S(1)} %get-tuple-element.37) | copy-start | bytes 24580
  258.7 136.1 %copy-start.10 = (f32[1,5,32768]{2,0,1:T(1,128)S(1)}, f32[1,5,32768]{2,0,1:T(1,128)}, u32[]{:S(2)}) copy-start(f32[1,5,32768]{2,0,1:T(1,128)} %all_gather.10) | copy-start | bytes 1966084
  258.7 136.1 %copy-start.11 = (f32[1,5,32768]{2,0,1:T(1,128)S(1)}, f32[1,5,32768]{2,0,1:T(1,128)}, u32[]{:S(2)}) copy-start(f32[1,5,32768]{2,0,1:T(1,128)} %all_gather.11) | copy-start | bytes 1966084
  263.2 135.1 %copy-start.48 = (s32[2048]{0:T(1024)S(1)}, s32[2048]{0:T(1024)}, u32[]{:S(2)}) copy-start(s32[2048]{0:T(1024)} %broadcast_clamp_fusion.4) | copy-start | bytes 24580
  398.2 5.8 %copy-start.9 = (f32[1,5,32768]{2,0,1:T(1,128)}, f32[1,5,32768]{2,0,1:T(1,128)S(1)}, u32[]{:S(2)}) copy-start(f32[1,5,32768]{2,0,1:T(1,128)S(1)} %get-tuple-element.16) | copy-start | bytes 1966084
  439.7 3.6 copy-start.25
  439.7 3.6 copy-start.27
  439.7 3.6 copy-start.39
  439.7 3.8 copy-start.23
  439.7 3.8 copy-start.37
  439.8 4.1 copy-start.21
  439.8 4.1 copy-start.35
  439.8 4.3 copy-start.33
  444.1 3.3 copy-start.12
  444.6 3.4 copy-start.13
  445.3 3.3 copy-start.14
  445.8 3.4 copy-start.15
  (21 other events, 41.8 us)
Sparse Core Ops, SparseCore 0:
  10.8 85.1 all-gather.1
  100.5 148.9 reduce-scatter.1
  258.8 135.9 all-reduce.1
where the time goes:
time: 460 us; the launch traced here: 459 us
  waiting for transfers between devices  265 us (58%)
  blocking collectives  78.3 us (17%)
  local copies, waits for them, and re-layouts  53.3 us (12%)
  matrix products  24 us (5%)
  other arithmetic  23.9 us (5%)
  between operations  14.5 us (3%)
    reduce_scatter x1, waiting for transfers between devices, on_device(): lax.psum_scatter(lax.dot_general(inputs, key_cotangent, contract_first, p...  133 us
    psum x1, waiting for transfers between devices, on_device(): total = lax.psum(local_table, 'dp')  132 us
    all_gather x1, blocking collectives, on_device(): lax.all_gather(momentum, 'dp', axis=2, tiled=True)  42.3 us
    gather x10, local copies, waits for them, and re-layouts, on_device(): error_rows[row_index][bucket[row_index]] * sign_values[row_index][:, None]  41.2 us
    all_gather x1, blocking collectives, on_device(): lax.all_gather(error, 'dp', axis=2, tiled=True)  36 us
  transfers between devices with their start and end apart: 3, of which 2 were waited for; matrix products, arithmetic and copies ran while one was open for 7% of the time, Pallas kernels for 0%

commit v1 on v0

--- a/solution.py
+++ b/solution.py
@@ -83,7 +83,7 @@
     ).reshape(1, ROWS, NBB * BLOCK)
     share = momentum.shape[2]
     offset = lax.axis_index("dp") * share
-    total = lax.psum(local_table, "dp")
+    total = jnp.sum(lax.all_gather(local_table, "dp"), axis=0)
     momentum_all, error_all = (
         lax.all_gather(momentum, "dp", axis=2, tiled=True),
         lax.all_gather(error, "dp", axis=2, tiled=True),

time: 460 us -> 454 us (0.987)
    psum x1 -> x0, waiting for transfers between devices: 132 us -> none  [on_device(): total = lax.psum(local_table, 'dp')]
    all_gather x0 -> x1, waiting for transfers between devices: none -> 106 us  [on_device(): total = jnp.sum(lax.all_gather(local_table, 'dp'), axis=0)]
    reduce_scatter x1, waiting for transfers between devices: 133 us -> 156 us  [on_device(): lax.psum_scatter(lax.dot_general(inputs, key_cotangent, contract_first, p...]
    reduce_sum x0 -> x1, other arithmetic: none -> 8.41 us  [on_device(): total = jnp.sum(lax.all_gather(local_table, 'dp'), axis=0)]
  transfers between devices with their start and end apart: 3 -> 3, of which waited for: 2 -> 2; matrix products, arithmetic and copies ran while one was open for 7% -> 5% of each run, Pallas kernels for 0% -> 0%
where the time goes in v1:
time: 454 us; the launch traced here: 452 us
  waiting for transfers between devices  262 us (58%)
  blocking collectives  74.9 us (16%)
  local copies, waits for them, and re-layouts  51.5 us (11%)
  other arithmetic  26.6 us (6%)
  matrix products  22.7 us (5%)
  between operations  14.5 us (3%)
    reduce_scatter x1, waiting for transfers between devices, on_device(): lax.psum_scatter(lax.dot_general(inputs, key_cotangent, contract_first, p...  156 us
    all_gather x1, waiting for transfers between devices, on_device(): total = jnp.sum(lax.all_gather(local_table, 'dp'), axis=0)  106 us
    gather x10, local copies, waits for them, and re-layouts, on_device(): error_rows[row_index][bucket[row_index]] * sign_values[row_index][:, None]  41.6 us
    all_gather x1, blocking collectives, on_device(): lax.all_gather(momentum, 'dp', axis=2, tiled=True)  39.1 us
    all_gather x1, blocking collectives, on_device(): lax.all_gather(error, 'dp', axis=2, tiled=True)  35.8 us
    dot_general x1, matrix products, on_device(): lax.dot_general(inputs, key_cotangent, contract_first, preferred_element_...  9.78 us
  transfers between devices with their start and end apart: 3, of which 2 were waited for; matrix products, arithmetic and copies ran while one was open for 5% of the time, Pallas kernels for 0%

profile of v1, /device:TPU:8, one launch (start us, length us, event | category | flops | bytes accessed | tf_op | source)
XLA Modules:
  0.0 452.4 jit_solution(17887697035218379490)
XLA Ops:
  7.2 2.1 fusion.10
  9.4 9.8 %fusion.11 = f32[8192,512]{1,0:T(8,128)} fusion(bf16[128,512]{1,0:T(8,128)(2,1)S(1)} %copy-done, bf16[128,8192]{1,0:T(8,128)(2,1)} %param.8, f32[8192]{0:T(1024)} %param.9, f32[128]{0:T(128)S(1)} %add_rsqrt_fusion), kind=kOutput, calls=%fused_computation.19 | convolution fusion | flops 1077936128 | bytes 19038720 | tf_op jit(solution)/shard_map/dot_general | solution.py:61
  19.2 0.7 all-gather.3.cloned.1.call-update
  20.2 155.5 %reduce-scatter.2.cloned.1.call-done = f32[512,512]{1,0:T(8,128)} async-done(((f32[8192,512]{1,0:T(8,128)}), f32[512,512]{1,0:T(8,128)}) %reduce-scatter.2.cloned.1.call-update) | async-done | bytes 1048592 | tf_op jit(solution)/shard_map/reduce_scatter | solution.py:60
  175.8 1.3 broadcast_multiply_fusion.1
  181.9 0.8 copy-done.16
  182.7 0.7 slice_reduce_fusion.7
  183.4 0.9 mul.191
  184.3 1.0 mul.195
  185.3 1.0 mul.199
  186.3 1.0 mul.203
  187.3 1.0 mul.207
  190.6 39.1 %all_gather.13 = f32[1,5,32768]{2,0,1:T(1,128)} all-gather(f32[1,5,2048]{2,0,1:T(1,128)S(1)} %copy-done.27), channel_id=1, replica_groups=mesh['dp'=16,'fsdp'=16] {'dp'}, dimensions={2}, use_global_device_ids=true | all-gather | bytes 696320 | tf_op jit(solution)/shard_map/all_gather | solution.py:88
  229.7 35.8 %all_gather.15 = f32[1,5,32768]{2,0,1:T(1,128)} all-gather(f32[1,5,2048]{2,0,1:T(1,128)S(1)} %copy-done.28), channel_id=1, replica_groups=mesh['dp'=16,'fsdp'=16] {'dp'}, dimensions={2}, use_global_device_ids=true | all-gather | bytes 696320 | tf_op jit(solution)/shard_map/all_gather | solution.py:89
  265.6 6.3 %fusion.5 = (f32[128]{0:T(128)S(1)}, f32[128,8192]{1,0:T(8,128)S(1)}) fusion(bf16[128,8192]{1,0:T(8,128)(2,1)S(1)} %copy-done.2, f32[128]{0:T(128)S(1)} %add_rsqrt_fusion, f32[8192]{0:T(1024)S(1)} %copy-done.17, bf16[128,512]{1,0:T(8,128)(2,1)S(1)} %copy-done, bf16[8192,512]{1,0:T(8,128)(2,1)} %all-gather.3.cloned.1.call-done), kind=kOutput, calls=%fused_computation.13 | convolution fusion | flops 1081081728 | bytes 14844928 | tf_op jit(solution)/shard_map/dot_general | solution.py:54
  271.9 2.3 fusion.8
  274.1 105.8 %all-gather.5.cloned.1.call-done = f32[16,1,5,32768]{3,1,2,0:T(1,128)} async-done(((f32[1,1,5,32768]{3,1,2,0:T(1,128)}), f32[16,1,5,32768]{3,1,2,0:T(1,128)}) %all-gather.5.cloned.1.call-update) | async-done | bytes 10485776 | tf_op jit(solution)/shard_map/all_gather | solution.py:86
  379.9 8.4 %reduce_sum.29 = f32[5,32768]{1,0:T(8,128)S(1)} reduce(f32[16,1,5,32768]{3,1,2,0:T(1,128)} %all-gather.5.cloned.1.call-done, f32[]{:T(128)} %constant.6.clone.1), dimensions={0,1}, to_apply=%region_3.4 | reduce | flops 2457600 | bytes 11141124 | tf_op jit(solution)/shard_map/reduce_sum | solution.py:86
  388.5 2.2 fusion.153
  390.7 5.5 %gather_fusion = f32[2048,128]{1,0:T(8,128)S(1)} fusion(f32[256,128]{1,0:T(8,128)S(1)} %bitcast.114, s32[2048]{0:T(1024)S(1)} %broadcast_clamp_fusion.4), kind=kCustom, calls=%fused_computation | custom fusion | bytes 2105344 | tf_op jit(solution)/shard_map/gather | solution.py:97
  396.2 1.2 gather.30
  397.4 5.5 %gather_fusion.1 = f32[2048,128]{1,0:T(8,128)S(1)} fusion(f32[256,128]{1,0:T(8,128)S(1)} %bitcast.113, s32[2048]{0:T(1024)S(1)} %broadcast_clamp_fusion.3), kind=kCustom, calls=%fused_computation.1 | custom fusion | bytes 2105344 | tf_op jit(solution)/shard_map/gather | solution.py:97
  402.8 1.1 gather.31
  404.0 6.4 %gather_fusion.2 = f32[2048,128]{1,0:T(8,128)S(1)} fusion(f32[256,128]{1,0:T(8,128)S(1)} %bitcast.112, s32[2048]{0:T(1024)} %broadcast_clamp_fusion.2), kind=kCustom, calls=%fused_computation.2 | custom fusion | bytes 2105344 | tf_op jit(solution)/shard_map/gather | solution.py:97
  410.4 1.1 gather.32
  411.5 8.4 %gather_fusion.3 = f32[2048,128]{1,0:T(8,128)} fusion(f32[256,128]{1,0:T(8,128)S(1)} %bitcast.111, s32[2048]{0:T(1024)} %broadcast_clamp_fusion.1), kind=kCustom, calls=%fused_computation.3 | custom fusion | bytes 2105344 | tf_op jit(solution)/shard_map/gather | solution.py:97
  420.0 2.3 gather.33
  422.3 7.6 %gather_fusion.4 = f32[2048,128]{1,0:T(8,128)} fusion(f32[256,128]{1,0:T(8,128)S(1)} %bitcast.110, s32[2048]{0:T(1024)S(1)} %copy-done.44), kind=kCustom, calls=%fused_computation.4 | custom fusion | bytes 2105344 | tf_op jit(solution)/shard_map/gather | solution.py:97
  430.0 2.4 gather.34
  432.4 3.5 subtract_convert_fusion
  438.6 1.9 dynamic-slice_subtract_fusion
  443.6 2.3 clamp_subtract_fusion
  (146 shorter events, 13.0 us)
Async XLA Ops:
  7.2 168.6 %reduce-scatter.2.cloned.1.call-start = ((), (), s32[]{:S(2)}) async-start(), calls=%async_computation.2 | async-start | bytes 17825792 | tf_op jit(solution)/shard_map/reduce_scatter | solution.py:60
  19.2 246.4 %all-gather.3.cloned.1.call-start = ((), (), s32[]{:S(2)}) async-start(), calls=%async_computation.1 | async-start | bytes 8912896 | tf_op jit(solution)/shard_map/all_gather | solution.py:56
  19.9 360.0 %all-gather.5.cloned.1.call-start = ((), (), s32[]{:S(2)}) async-start(), calls=%async_computation.3 | async-start | bytes 11141120 | tf_op jit(solution)/shard_map/all_gather | solution.py:86
  20.1 157.6 %copy-start.29 = (bf16[2048]{0:T(1024)(128)(2,1)}, bf16[2048]{0:T(1024)(128)(2,1)S(1)}, u32[]{:S(2)}) copy-start(bf16[2048]{0:T(1024)(128)(2,1)S(1)} %get-tuple-element.13) | copy-start | bytes 12292
  20.1 159.8 %copy-start.31 = (bf16[2048]{0:T(1024)(128)(2,1)}, bf16[2048]{0:T(1024)(128)(2,1)S(1)}, u32[]{:S(2)}) copy-start(bf16[2048]{0:T(1024)(128)(2,1)S(1)} %get-tuple-element.12) | copy-start | bytes 12292
  20.1 160.2 %copy-start.33 = (bf16[2048]{0:T(1024)(128)(2,1)}, bf16[2048]{0:T(1024)(128)(2,1)S(1)}, u32[]{:S(2)}) copy-start(bf16[2048]{0:T(1024)(128)(2,1)S(1)} %get-tuple-element.11) | copy-start | bytes 12292
  20.2 160.7 %copy-start.35 = (bf16[2048]{0:T(1024)(128)(2,1)}, bf16[2048]{0:T(1024)(128)(2,1)S(1)}, u32[]{:S(2)}) copy-start(bf16[2048]{0:T(1024)(128)(2,1)S(1)} %get-tuple-element.10) | copy-start | bytes 12292
  20.2 161.1 %copy-start.37 = (bf16[2048]{0:T(1024)(128)(2,1)}, bf16[2048]{0:T(1024)(128)(2,1)S(1)}, u32[]{:S(2)}) copy-start(bf16[2048]{0:T(1024)(128)(2,1)S(1)} %get-tuple-element.9) | copy-start | bytes 12292
  20.2 160.2 %copy-start.19 = (s32[1,2048]{1,0:T(1,128)}, s32[1,2048]{1,0:T(1,128)S(1)}, u32[]{:S(2)}) copy-start(s32[1,2048]{1,0:T(1,128)S(1)} %get-tuple-element.38) | copy-start | bytes 24580
  20.2 160.6 %copy-start.21 = (s32[1,2048]{1,0:T(1,128)}, s32[1,2048]{1,0:T(1,128)S(1)}, u32[]{:S(2)}) copy-start(s32[1,2048]{1,0:T(1,128)S(1)} %get-tuple-element.41) | copy-start | bytes 24580
  20.2 161.1 %copy-start.23 = (s32[1,2048]{1,0:T(1,128)}, s32[1,2048]{1,0:T(1,128)S(1)}, u32[]{:S(2)}) copy-start(s32[1,2048]{1,0:T(1,128)S(1)} %get-tuple-element.37) | copy-start | bytes 24580
  180.8 9.8 %copy-start.27 = (f32[1,5,2048]{2,0,1:T(1,128)S(1)}, f32[1,5,2048]{2,0,1:T(1,128)}, u32[]{:S(2)}) copy-start(f32[1,5,2048]{2,0,1:T(1,128)} %param.14) | copy-start | bytes 122884
  180.8 48.9 %copy-start.28 = (f32[1,5,2048]{2,0,1:T(1,128)S(1)}, f32[1,5,2048]{2,0,1:T(1,128)}, u32[]{:S(2)}) copy-start(f32[1,5,2048]{2,0,1:T(1,128)} %param.15) | copy-start | bytes 122884
  181.3 84.2 %copy-start.2 = (bf16[128,8192]{1,0:T(8,128)(2,1)S(1)}, bf16[128,8192]{1,0:T(8,128)(2,1)}, u32[]{:S(2)}) copy-start(bf16[128,8192]{1,0:T(8,128)(2,1)} %param.8) | copy-start | bytes 6291460
  181.3 84.2 %copy-start.17 = (f32[8192]{0:T(1024)S(1)}, f32[8192]{0:T(1024)}, u32[]{:S(2)}) copy-start(f32[8192]{0:T(1024)} %param.9) | copy-start | bytes 98308
  274.1 114.3 %copy-start.9 = (f32[1,5,32768]{2,0,1:T(1,128)S(1)}, f32[1,5,32768]{2,0,1:T(1,128)}, u32[]{:S(2)}) copy-start(f32[1,5,32768]{2,0,1:T(1,128)} %all_gather.13) | copy-start | bytes 1966084
  274.1 114.3 %copy-start.10 = (f32[1,5,32768]{2,0,1:T(1,128)S(1)}, f32[1,5,32768]{2,0,1:T(1,128)}, u32[]{:S(2)}) copy-start(f32[1,5,32768]{2,0,1:T(1,128)} %all_gather.15) | copy-start | bytes 1966084
  411.5 10.8 %copy-start.44 = (s32[2048]{0:T(1024)S(1)}, s32[2048]{0:T(1024)}, u32[]{:S(2)}) copy-start(s32[2048]{0:T(1024)} %broadcast_clamp_fusion) | copy-start | bytes 24580
  422.3 10.1 %copy-start.39 = (f32[1,2048]{1,0:T(1,128)S(1)}, f32[1,2048]{1,0:T(1,128)}, u32[]{:S(2)}) copy-start(f32[1,2048]{1,0:T(1,128)} %get-tuple-element.25) | copy-start | bytes 24580
  422.3 10.1 %copy-start.40 = (f32[1,2048]{1,0:T(1,128)S(1)}, f32[1,2048]{1,0:T(1,128)}, u32[]{:S(2)}) copy-start(f32[1,2048]{1,0:T(1,128)} %get-tuple-element.26) | copy-start | bytes 24580
  422.3 10.1 %copy-start.41 = (f32[1,2048]{1,0:T(1,128)S(1)}, f32[1,2048]{1,0:T(1,128)}, u32[]{:S(2)}) copy-start(f32[1,2048]{1,0:T(1,128)} %get-tuple-element.27) | copy-start | bytes 24580
  422.3 10.1 %copy-start.42 = (f32[1,2048]{1,0:T(1,128)S(1)}, f32[1,2048]{1,0:T(1,128)}, u32[]{:S(2)}) copy-start(f32[1,2048]{1,0:T(1,128)} %get-tuple-element.28) | copy-start | bytes 24580
  422.3 10.1 %copy-start.43 = (f32[1,2048]{1,0:T(1,128)S(1)}, f32[1,2048]{1,0:T(1,128)}, u32[]{:S(2)}) copy-start(f32[1,2048]{1,0:T(1,128)} %get-tuple-element.29) | copy-start | bytes 24580
  430.0 6.0 %copy-start.24 = (s32[1,2048]{1,0:T(1,128)S(1)}, s32[1,2048]{1,0:T(1,128)}, u32[]{:S(2)}) copy-start(s32[1,2048]{1,0:T(1,128)} %copy-done.23) | copy-start | bytes 24580
  430.0 6.0 %copy-start.26 = (s32[16]{0:T(128)S(1)}, s32[16]{0:T(128)}, u32[]{:S(2)}) copy-start(s32[16]{0:T(128)} %fusion.132) | copy-start | bytes 196
  430.0 6.0 %copy-start.38 = (bf16[2048]{0:T(1024)(128)(2,1)S(1)}, bf16[2048]{0:T(1024)(128)(2,1)}, u32[]{:S(2)}) copy-start(bf16[2048]{0:T(1024)(128)(2,1)} %copy-done.37) | copy-start | bytes 12292
  430.0 6.3 %copy-start.22 = (s32[1,2048]{1,0:T(1,128)S(1)}, s32[1,2048]{1,0:T(1,128)}, u32[]{:S(2)}) copy-start(s32[1,2048]{1,0:T(1,128)} %copy-done.21) | copy-start | bytes 24580
  430.0 6.3 %copy-start.36 = (bf16[2048]{0:T(1024)(128)(2,1)S(1)}, bf16[2048]{0:T(1024)(128)(2,1)}, u32[]{:S(2)}) copy-start(bf16[2048]{0:T(1024)(128)(2,1)} %copy-done.35) | copy-start | bytes 12292
  436.5 5.8 %copy-start.14 = (f32[512,4]{1,0:T(8,128)S(1)}, f32[512,4]{1,0:T(8,128)}, u32[]{:S(2)}) copy-start(f32[512,4]{1,0:T(8,128)} %mul.203) | copy-start | bytes 24580
  437.8 5.8 %copy-start.4 = (f32[512,512]{1,0:T(8,128)S(1)}, f32[512,512]{1,0:T(8,128)}, u32[]{:S(2)}) copy-start(f32[512,512]{1,0:T(8,128)} %gather.31) | copy-start | bytes 3145732
  437.8 5.8 %copy-start.5 = (f32[512,512]{1,0:T(8,128)S(1)}, f32[512,512]{1,0:T(8,128)}, u32[]{:S(2)}) copy-start(f32[512,512]{1,0:T(8,128)} %gather.32) | copy-start | bytes 3145732
  437.8 5.8 %copy-start.6 = (f32[512,512]{1,0:T(8,128)S(1)}, f32[512,512]{1,0:T(8,128)}, u32[]{:S(2)}) copy-start(f32[512,512]{1,0:T(8,128)} %gather.33) | copy-start | bytes 3145732
  (16 other events, 62.5 us)
Sparse Core Ops, SparseCore 0:
  19.3 156.4 reduce-scatter.1
  178.5 80.8 all-gather.2
  261.7 118.1 all-gather.4
